TPU v7x, 32 devices: a whole 2x2x4 slice. The times are simulated.
32 devices in a mesh: dp: 8 (over y, x, core), expert: 4 (over z).
Axes of the slice: x: 2, y: 2, z: 4, core: 2. Of those that a mesh axis runs over, the one named last changes fastest.
Arguments:
- tokens: bfloat16 [4096, 1024], P(('dp', 'expert')), may hold values from -24 to 24
- route_first: int32 [4096, 1], P(('dp', 'expert')), may hold values from 0 to 1; in each aligned block of 128 rows (0 to 127, 128 to 255, ...) at most 68 rows name the same one
- route_second: int32 [4096, 1], P(('dp', 'expert')), may hold values from 0 to 1; in each aligned block of 128 rows (0 to 127, 128 to 255, ...) at most 68 rows name the same one
- up_first: bfloat16 [4, 1024, 2048], P('expert', 'dp'), may hold values from -0.1875 to 0.1875
- down_first: bfloat16 [4, 2048, 1024], P('expert', 'dp'), may hold values from -0.09375 to 0.09375
- up_second: bfloat16 [4, 1024, 2048], P('expert', 'dp'), may hold values from -0.1875 to 0.1875
- down_second: bfloat16 [4, 2048, 1024], P('expert', 'dp'), may hold values from -0.09375 to 0.09375
- cotangent: bfloat16 [4096, 1024], P(('dp', 'expert')), may hold values from -6 to 6
Outputs:
- layer_out: bfloat16 [4096, 1024], P(('dp', 'expert'))
- grad_tokens: bfloat16 [4096, 1024], P(('dp', 'expert'))
- grad_up_first: float32 [4, 1024, 2048], P('expert', 'dp')
- grad_down_first: float32 [4, 2048, 1024], P('expert', 'dp')
- grad_up_second: float32 [4, 1024, 2048], P('expert', 'dp')
- grad_down_second: float32 [4, 2048, 1024], P('expert', 'dp')
Inputs may be any that keep to these rules, and one draw needn't show every extreme that they name: `route_first`: in each aligned block of 128 rows (the rows of one device) no expert id appears more than 68 times, and in every draw some expert appears exactly 68 times in some block. `route_second`: in each aligned block of 128 rows (the rows of one device) no expert id appears more than 68 times, and in every draw some expert appears exactly 68 times in some block.
All inputs are finite; a program needn't handle non-finite values.
Results may differ from a plain program's by a relative error of at most 0.025.
Values may be sent and summed in bfloat16 or wider, within the bound.
A program may use at most 128 MiB of HBM per device.

v0:
```python
import jax
import jax.numpy as jnp
from jax import lax
from jax.sharding import PartitionSpec as P

epsilon = 1e-06


def rms_normal(widened):
    return widened * lax.rsqrt(jnp.mean(widened * widened, axis=-1, keepdims=True) + epsilon)


def gelu_slope(pre_gelu):
    _, pullback = jax.vjp(jax.nn.gelu, pre_gelu)
    return pullback(jnp.ones_like(pre_gelu))[0]


def slot_places(route_ids, experts, capacity):
    expert_ids = route_ids[:, 0]
    onehot = (expert_ids[:, None] == jnp.arange(experts, dtype=jnp.int32)[None, :]).astype(
        jnp.int32
    )
    earlier = jnp.cumsum(onehot, axis=0) - onehot
    return expert_ids * capacity + jnp.sum(earlier * onehot, axis=1)


def to_slots(token_rows, places, slot_count):
    onehot_table = (places[None, :] == jnp.arange(slot_count, dtype=jnp.int32)[:, None]).astype(
        token_rows.dtype
    )
    return jnp.dot(onehot_table, token_rows, preferred_element_type=jnp.float32).astype(
        token_rows.dtype
    )


def from_slots(returned, places, experts):
    group_size = returned.shape[0] // experts
    feature_count = returned.shape[2]
    summed = (
        returned.reshape(experts, group_size, returned.shape[1], feature_count)
        .astype(jnp.float32)
        .sum(axis=1)
    )
    summed = summed.reshape(-1, feature_count)
    onehot_table = (
        places[:, None] == jnp.arange(summed.shape[0], dtype=jnp.int32)[None, :]
    ).astype(jnp.float32)
    return jnp.dot(
        onehot_table, summed, precision=lax.Precision.HIGHEST, preferred_element_type=jnp.float32
    )


def moe_forward(token_rows, route_ids, weights, experts, capacity):
    up_full, down_full = weights
    group_size = lax.axis_size("expert") // experts
    places = slot_places(route_ids, experts, capacity)
    widened = token_rows.astype(jnp.float32)
    normed = rms_normal(widened).astype(jnp.bfloat16)
    slot_rows = to_slots(normed, places, experts * capacity).reshape(experts, capacity, -1)
    outgoing = jnp.repeat(slot_rows, group_size, axis=0)
    received = lax.all_to_all(outgoing, "expert", split_axis=0, concat_axis=0, tiled=True)
    pre_gelu = jnp.einsum("skd,dh->skh", received, up_full, preferred_element_type=jnp.float32)
    hidden = jax.nn.gelu(pre_gelu).astype(jnp.bfloat16)
    partial_out = jnp.einsum(
        "skh,hd->skd", hidden, down_full, preferred_element_type=jnp.float32
    ).astype(jnp.bfloat16)
    returned = lax.all_to_all(partial_out, "expert", split_axis=0, concat_axis=0, tiled=True)
    returned, received, pre_gelu, hidden = (returned, received, pre_gelu, hidden)
    branch = from_slots(returned, places, experts)
    layer_out = (widened + branch).astype(jnp.bfloat16)
    return (layer_out, (widened, places, received, pre_gelu, hidden))


def moe_backward(upstream, saved, weights, experts, capacity):
    up_full, down_full = weights
    widened, places, received, pre_gelu, hidden = saved
    group_size = lax.axis_size("expert") // experts
    slot_rows = to_slots(upstream, places, experts * capacity).reshape(experts, capacity, -1)
    outgoing = jnp.repeat(slot_rows, group_size, axis=0)
    arriving = lax.all_to_all(outgoing, "expert", split_axis=0, concat_axis=0, tiled=True)
    grad_hidden = jnp.einsum("skd,hd->skh", arriving, down_full, preferred_element_type=jnp.float32)
    grad_pre = (grad_hidden * gelu_slope(pre_gelu)).astype(jnp.bfloat16)
    grad_down = jnp.einsum("skh,skd->hd", hidden, arriving, preferred_element_type=jnp.float32)
    grad_up = jnp.einsum("skd,skh->dh", received, grad_pre, preferred_element_type=jnp.float32)
    grad_slots = jnp.einsum(
        "skh,dh->skd", grad_pre, up_full, preferred_element_type=jnp.float32
    ).astype(jnp.bfloat16)
    coming_back = lax.all_to_all(grad_slots, "expert", split_axis=0, concat_axis=0, tiled=True)
    grad_normed = from_slots(coming_back, places, experts)
    _, pullback = jax.vjp(rms_normal, widened)
    grad_input = (upstream.astype(jnp.float32) + pullback(grad_normed)[0]).astype(jnp.bfloat16)
    return (grad_input, grad_up, grad_down)


def fetch_layer(up_shard, down_shard):
    up_full, down_full = (
        lax.all_gather(up_shard, "dp", axis=1, tiled=True),
        lax.all_gather(down_shard, "dp", axis=1, tiled=True),
    )
    return (up_full[0], down_full[0])


def capacity_for(token_count, experts):
    return min(token_count, (token_count * 17 + 16 * experts - 1) // (16 * experts))


def local(
    tokens, route_first, route_second, up_first, down_first, up_second, down_second, cotangent
):
    expert_devices = lax.axis_size("expert")
    token_count = tokens.shape[0]
    experts_first = max(expert_devices // 4, 2)
    experts_second = max(expert_devices // 2, 2)
    cap_first = capacity_for(token_count, experts_first)
    cap_second = capacity_for(token_count, experts_second)
    first_weights = fetch_layer(up_first, down_first)
    middle, first_saved = moe_forward(tokens, route_first, first_weights, experts_first, cap_first)
    second_weights = fetch_layer(up_second, down_second)
    layer_out, second_saved = moe_forward(
        middle, route_second, second_weights, experts_second, cap_second
    )
    grad_middle, up_grad_second, down_grad_second = moe_backward(
        cotangent, second_saved, second_weights, experts_second, cap_second
    )
    grad_tokens, up_grad_first, down_grad_first = moe_backward(
        grad_middle, first_saved, first_weights, experts_first, cap_first
    )
    reduced_all = (
        lax.psum_scatter(
            up_grad_first.astype(jnp.bfloat16), "dp", scatter_dimension=0, tiled=True
        ).astype(jnp.float32),
        lax.psum_scatter(
            down_grad_first.astype(jnp.bfloat16), "dp", scatter_dimension=0, tiled=True
        ).astype(jnp.float32),
        lax.psum_scatter(
            up_grad_second.astype(jnp.bfloat16), "dp", scatter_dimension=0, tiled=True
        ).astype(jnp.float32),
        lax.psum_scatter(
            down_grad_second.astype(jnp.bfloat16), "dp", scatter_dimension=0, tiled=True
        ).astype(jnp.float32),
    )
    reduced_first = (reduced_all[0][None], reduced_all[1][None])
    reduced_second = (reduced_all[2][None], reduced_all[3][None])
    return (
        layer_out,
        grad_tokens,
        reduced_first[0],
        reduced_first[1],
        reduced_second[0],
        reduced_second[1],
    )


def solution(mesh):
    in_specs = (
        P(("dp", "expert"), None),
        P(("dp", "expert"), None),
        P(("dp", "expert"), None),
        P("expert", "dp", None),
        P("expert", "dp", None),
        P("expert", "dp", None),
        P("expert", "dp", None),
        P(("dp", "expert"), None),
    )
    out_specs = (
        P(("dp", "expert"), None),
        P(("dp", "expert"), None),
        P("expert", "dp", None),
        P("expert", "dp", None),
        P("expert", "dp", None),
        P("expert", "dp", None),
    )
    return jax.shard_map(local, mesh=mesh, in_specs=in_specs, out_specs=out_specs, check_vma=False)
```

profile of v0, /device:TPU:0, one launch (start us, length us, event | category | flops | bytes accessed | tf_op | source)
XLA Modules:
  0.0 391.4 jit_solution(15165776641200800257)
XLA Ops:
  12.4 22.0 %all_to_all.40 = bf16[4,68,1024]{2,1,0:T(8,128)(2,1)S(1)} all-to-all(bf16[4,68,1024]{2,1,0:T(8,128)(2,1)S(1)} %bitcast.110), channel_id=1, replica_groups=mesh['dp'=8,'expert'=4] {'expert'}, dimensions={0} | all-to-all | bytes 1114112 | tf_op jit(solution)/shard_map/all_to_all | solution.py:61
  34.4 14.8 %all-gather.5.cloned.1.call-done = bf16[1,1024,2048]{2,1,0:T(8,128)(2,1)} async-done(((bf16[1,128,2048]{2,1,0:T(8,128)(2,1)}), bf16[1,1024,2048]{2,1,0:T(8,128)(2,1)}) %all-gather.5.cloned.1.call-update) | async-done | bytes 4194320 | tf_op jit(solution)/shard_map/all_gather | solution.py:97
  49.2 5.0 %fusion.14 = f32[4,68,2048]{2,1,0:T(8,128)} fusion(bf16[4,68,1024]{2,1,0:T(8,128)(2,1)S(1)} %all_to_all.40, bf16[1,1024,2048]{2,1,0:T(8,128)(2,1)} %all-gather.5.cloned.1.call-done), kind=kOutput, calls=%fused_computation.18 | convolution fusion | flops 1140850688 | bytes 6979584 | tf_op jit(solution)/shard_map/skd,dh->skh/dot_general | solution.py:62
  54.3 33.5 %all-gather.7.cloned.1.call-done = bf16[1,2048,1024]{2,1,0:T(8,128)(2,1)} async-done(((bf16[1,256,1024]{2,1,0:T(8,128)(2,1)}), bf16[1,2048,1024]{2,1,0:T(8,128)(2,1)}) %all-gather.7.cloned.1.call-update) | async-done | bytes 4194320 | tf_op jit(solution)/shard_map/all_gather | solution.py:98
  87.7 5.5 %fusion.43 = bf16[4,68,1024]{2,1,0:T(8,128)(2,1)} fusion(bf16[1,2048,1024]{2,1,0:T(8,128)(2,1)} %all-gather.7.cloned.1.call-done, f32[4,68,2048]{2,1,0:T(8,128)} %fusion.14), kind=kOutput, calls=%fused_computation.43 | convolution fusion | flops 1146142720 | bytes 6979584 | tf_op jit(solution)/shard_map/skh,hd->skd/dot_general | solution.py:64
  93.2 4.6 %all-to-all-start.1 = ((bf16[4,68,1024]{2,1,0:T(8,128)(2,1)}), bf16[4,68,1024]{2,1,0:T(8,128)(2,1)S(1)}, u32[]{:S(2)}, u32[]{:S(2)}) async-start(bf16[4,68,1024]{2,1,0:T(8,128)(2,1)} %fusion.43), calls=%async_computation.1 | async-start | bytes 1179648 | tf_op jit(solution)/shard_map/all_to_all | solution.py:67
  98.3 15.8 %all-to-all-done.1 = bf16[4,68,1024]{2,1,0:T(8,128)(2,1)S(1)} async-done(((bf16[4,68,1024]{2,1,0:T(8,128)(2,1)}), bf16[4,68,1024]{2,1,0:T(8,128)(2,1)S(1)}, u32[]{:S(2)}, u32[]{:S(2)}) %all-to-all-start.1) | async-done | bytes 557088 | tf_op jit(solution)/shard_map/all_to_all | solution.py:67
  119.9 15.1 %all-to-all-done.2 = bf16[4,68,1024]{2,1,0:T(8,128)(2,1)S(1)} async-done(((bf16[4,68,1024]{2,1,0:T(8,128)(2,1)}), bf16[4,68,1024]{2,1,0:T(8,128)(2,1)S(1)}, u32[]{:S(2)}, u32[]{:S(2)}) %all-to-all-start.2) | async-done | bytes 557088 | tf_op jit(solution)/shard_map/all_to_all | solution.py:61
  139.5 5.1 %fusion.6 = f32[4,68,2048]{2,1,0:T(8,128)} fusion(bf16[4,68,1024]{2,1,0:T(8,128)(2,1)S(1)} %all-to-all-done.2, bf16[1,1024,2048]{2,1,0:T(8,128)(2,1)} %all-gather.9.cloned.1.call-done), kind=kOutput, calls=%fused_computation.10 | convolution fusion | flops 1140850688 | bytes 6979584 | tf_op jit(solution)/shard_map/skd,dh->skh/dot_general | solution.py:62
  144.5 10.3 %all-to-all-done.4 = bf16[4,68,1024]{2,1,0:T(8,128)(2,1)S(1)} async-done(((bf16[4,68,1024]{2,1,0:T(8,128)(2,1)}), bf16[4,68,1024]{2,1,0:T(8,128)(2,1)S(1)}, u32[]{:S(2)}, u32[]{:S(2)}) %all-to-all-start.4) | async-done | bytes 557088 | tf_op jit(solution)/shard_map/all_to_all | solution.py:80
  154.8 6.3 %bitcast_convert_fusion = bf16[2048,1024]{1,0:T(8,128)(2,1)} fusion(bf16[4,68,1024]{2,1,0:T(8,128)(2,1)S(1)} %all-to-all-done.4, f32[4,68,2048]{2,1,0:T(8,128)} %fusion.6), kind=kOutput, calls=%fused_computation | convolution fusion | flops 1147961344 | bytes 6979584 | tf_op jit(solution)/shard_map/skh,skd->hd/dot_general | solution.py:83
  164.6 5.5 %fusion.22 = bf16[4,68,2048]{2,1,0:T(8,128)(2,1)S(1)} fusion(bf16[4,68,1024]{2,1,0:T(8,128)(2,1)S(1)} %all-to-all-done.4, bf16[1,2048,1024]{2,1,0:T(8,128)(2,1)} %all-gather.11.cloned.1.call-done, f32[4,68,2048]{2,1,0:T(8,128)} %fusion.6), kind=kOutput, calls=%fused_computation.26 | convolution fusion | flops 1151434752 | bytes 8093696 | tf_op jit(solution)/shard_map/skd,hd->skh/dot_general | solution.py:81
  176.9 4.8 %fusion.46 = bf16[4,68,1024]{2,1,0:T(8,128)(2,1)} fusion(bf16[4,68,2048]{2,1,0:T(8,128)(2,1)S(1)} %copy-done.9, bf16[1,1024,2048]{2,1,0:T(8,128)(2,1)} %all-gather.9.cloned.1.call-done), kind=kOutput, calls=%fused_computation.44 | convolution fusion | flops 1141129216 | bytes 5865472 | tf_op jit(solution)/shard_map/skh,dh->skd/dot_general | solution.py:85
  181.7 4.6 %all-to-all-start.5 = ((bf16[4,68,1024]{2,1,0:T(8,128)(2,1)}), bf16[4,68,1024]{2,1,0:T(8,128)(2,1)S(1)}, u32[]{:S(2)}, u32[]{:S(2)}) async-start(bf16[4,68,1024]{2,1,0:T(8,128)(2,1)} %fusion.46), calls=%async_computation.5 | async-start | bytes 1179648 | tf_op jit(solution)/shard_map/all_to_all | solution.py:88
  186.3 16.4 %all-to-all-done.5 = bf16[4,68,1024]{2,1,0:T(8,128)(2,1)S(1)} async-done(((bf16[4,68,1024]{2,1,0:T(8,128)(2,1)}), bf16[4,68,1024]{2,1,0:T(8,128)(2,1)S(1)}, u32[]{:S(2)}, u32[]{:S(2)}) %all-to-all-start.5) | async-done | bytes 557088 | tf_op jit(solution)/shard_map/all_to_all | solution.py:88
  203.9 17.9 %all_to_all.41 = bf16[4,68,1024]{2,1,0:T(8,128)(2,1)S(1)} all-to-all(bf16[4,68,1024]{2,1,0:T(8,128)(2,1)S(1)} %bitcast.111), channel_id=1, replica_groups=mesh['dp'=8,'expert'=4] {'expert'}, dimensions={0} | all-to-all | bytes 1114112 | tf_op jit(solution)/shard_map/all_to_all | solution.py:80
  221.8 5.7 %fusion.25 = bf16[4,68,2048]{2,1,0:T(8,128)(2,1)S(1)} fusion(bf16[4,68,1024]{2,1,0:T(8,128)(2,1)S(1)} %all_to_all.41, bf16[1,2048,1024]{2,1,0:T(8,128)(2,1)} %all-gather.7.cloned.1.call-done, f32[4,68,2048]{2,1,0:T(8,128)} %fusion.14), kind=kOutput, calls=%fused_computation.27 | convolution fusion | flops 1151434752 | bytes 8093696 | tf_op jit(solution)/shard_map/skd,hd->skh/dot_general | solution.py:81
  234.8 5.7 %bitcast_convert_fusion.2 = bf16[2048,1024]{1,0:T(8,128)(2,1)} fusion(bf16[4,68,1024]{2,1,0:T(8,128)(2,1)} %copy-done.4, f32[4,68,2048]{2,1,0:T(8,128)S(1)} %copy-done.1), kind=kOutput, calls=%fused_computation.2 | convolution fusion | flops 1147961344 | bytes 6979584 | tf_op jit(solution)/shard_map/skh,skd->hd/dot_general | solution.py:83
  242.1 4.9 %fusion.49 = bf16[4,68,1024]{2,1,0:T(8,128)(2,1)} fusion(bf16[1,2048,1024]{2,1,0:T(8,128)(2,1)} %all-gather.11.cloned.1.call-done, f32[4,68,2048]{2,1,0:T(8,128)S(1)} %copy-done.2), kind=kOutput, calls=%fused_computation.45 | convolution fusion | flops 1146142720 | bytes 6979584 | tf_op jit(solution)/shard_map/skh,hd->skd/dot_general | solution.py:64
  250.5 4.8 %fusion.40 = bf16[4,68,1024]{2,1,0:T(8,128)(2,1)} fusion(bf16[4,68,2048]{2,1,0:T(8,128)(2,1)} %copy-done.7, bf16[1,1024,2048]{2,1,0:T(8,128)(2,1)} %all-gather.5.cloned.1.call-done), kind=kOutput, calls=%fused_computation.42 | convolution fusion | flops 1141129216 | bytes 5865472 | tf_op jit(solution)/shard_map/skh,dh->skd/dot_general | solution.py:85
  255.3 10.4 %all-to-all-done.3 = bf16[4,68,1024]{2,1,0:T(8,128)(2,1)S(1)} async-done(((bf16[4,68,1024]{2,1,0:T(8,128)(2,1)}), bf16[4,68,1024]{2,1,0:T(8,128)(2,1)S(1)}, u32[]{:S(2)}, u32[]{:S(2)}) %all-to-all-start.3) | async-done | bytes 557088 | tf_op jit(solution)/shard_map/all_to_all | solution.py:67
  270.5 14.1 %all-to-all-done.7 = bf16[4,68,1024]{2,1,0:T(8,128)(2,1)S(1)} async-done(((bf16[4,68,1024]{2,1,0:T(8,128)(2,1)}), bf16[4,68,1024]{2,1,0:T(8,128)(2,1)S(1)}, u32[]{:S(2)}, u32[]{:S(2)}) %all-to-all-start.7) | async-done | bytes 557088 | tf_op jit(solution)/shard_map/all_to_all | solution.py:88
  290.6 37.3 %reduce-scatter.5.cloned.1.call-done = bf16[128,2048]{1,0:T(8,128)(2,1)} async-done(((bf16[1024,2048]{1,0:T(8,128)(2,1)}), bf16[128,2048]{1,0:T(8,128)(2,1)}) %reduce-scatter.5.cloned.1.call-update) | async-done | bytes 524304 | tf_op jit(solution)/shard_map/reduce_scatter | solution.py:129
  330.0 52.4 %reduce-scatter.7.cloned.1.call-done = bf16[256,1024]{1,0:T(8,128)(2,1)} async-done(((bf16[2048,1024]{1,0:T(8,128)(2,1)}), bf16[256,1024]{1,0:T(8,128)(2,1)}) %reduce-scatter.7.cloned.1.call-update) | async-done | bytes 524304 | tf_op jit(solution)/shard_map/reduce_scatter | solution.py:132
  (91 shorter events, 54.4 us)
Async XLA Ops:
  7.2 4.7 %copy-start.5 = (s32[128,1]{0,1:T(1,128)S(1)}, s32[128,1]{0,1:T(1,128)}, u32[]{:S(2)}) copy-start(s32[128,1]{0,1:T(1,128)} %param.9) | copy-start | bytes 1540
  7.2 4.6 %copy-start = (bf16[128,1024]{1,0:T(8,128)(2,1)S(1)}, bf16[128,1024]{1,0:T(8,128)(2,1)}, u32[]{:S(2)}) copy-start(bf16[128,1024]{1,0:T(8,128)(2,1)} %param.8) | copy-start | bytes 786436
  7.2 42.0 %all-gather.5.cloned.1.call-start = ((), (), s32[]{:S(2)}) async-start(), calls=%async_computation.12 | async-start | bytes 4718592 | tf_op jit(solution)/shard_map/all_gather | solution.py:97
  7.9 79.8 %all-gather.7.cloned.1.call-start = ((), (), s32[]{:S(2)}) async-start(), calls=%async_computation.13 | async-start | bytes 4718592 | tf_op jit(solution)/shard_map/all_gather | solution.py:98
  8.7 130.8 %all-gather.9.cloned.1.call-start = ((), (), s32[]{:S(2)}) async-start(), calls=%async_computation.14 | async-start | bytes 4718592 | tf_op jit(solution)/shard_map/all_gather | solution.py:97
  9.4 155.2 %all-gather.11.cloned.1.call-start = ((), (), s32[]{:S(2)}) async-start(), calls=%async_computation.15 | async-start | bytes 4718592 | tf_op jit(solution)/shard_map/all_gather | solution.py:98
  54.3 43.6 %copy-start.6 = (s32[128,1]{0,1:T(1,128)S(1)}, s32[128,1]{0,1:T(1,128)}, u32[]{:S(2)}) copy-start(s32[128,1]{0,1:T(1,128)} %param.10) | copy-start | bytes 1540
  93.2 20.9 %all-to-all-start.1 = ((bf16[4,68,1024]{2,1,0:T(8,128)(2,1)}), bf16[4,68,1024]{2,1,0:T(8,128)(2,1)S(1)}, u32[]{:S(2)}, u32[]{:S(2)}) async-start(bf16[4,68,1024]{2,1,0:T(8,128)(2,1)} %fusion.43), calls=%async_computation.1 | async-start | bytes 1179648 | tf_op jit(solution)/shard_map/all_to_all | solution.py:67
  114.3 5.3 %copy-start.3 = (bf16[128,1024]{1,0:T(8,128)(2,1)S(1)}, bf16[128,1024]{1,0:T(8,128)(2,1)}, u32[]{:S(2)}) copy-start(bf16[128,1024]{1,0:T(8,128)(2,1)} %param.15) | copy-start | bytes 786436
  116.1 18.9 %all-to-all-start.2 = ((bf16[4,68,1024]{2,1,0:T(8,128)(2,1)}), bf16[4,68,1024]{2,1,0:T(8,128)(2,1)S(1)}, u32[]{:S(2)}, u32[]{:S(2)}) async-start(bf16[4,68,1024]{2,1,0:T(8,128)(2,1)} %bitcast.12), calls=%async_computation.2 | async-start | bytes 1179648 | tf_op jit(solution)/shard_map/all_to_all | solution.py:61
  135.9 18.9 %all-to-all-start.4 = ((bf16[4,68,1024]{2,1,0:T(8,128)(2,1)}), bf16[4,68,1024]{2,1,0:T(8,128)(2,1)S(1)}, u32[]{:S(2)}, u32[]{:S(2)}) async-start(bf16[4,68,1024]{2,1,0:T(8,128)(2,1)} %bitcast.18), calls=%async_computation.4 | async-start | bytes 1179648 | tf_op jit(solution)/shard_map/all_to_all | solution.py:80
  139.4 146.8 %reduce-scatter.11.cloned.1.call-start = ((), (), s32[]{:S(2)}) async-start(), calls=%async_computation.19 | async-start | bytes 4718592 | tf_op jit(solution)/shard_map/reduce_scatter | solution.py:138
  161.2 127.2 %reduce-scatter.9.cloned.1.call-start = ((), (), s32[]{:S(2)}) async-start(), calls=%async_computation.18 | async-start | bytes 4718592 | tf_op jit(solution)/shard_map/reduce_scatter | solution.py:135
  170.1 1.0 copy-start.8
  175.5 1.4 copy-start.9
  181.7 21.0 %all-to-all-start.5 = ((bf16[4,68,1024]{2,1,0:T(8,128)(2,1)}), bf16[4,68,1024]{2,1,0:T(8,128)(2,1)S(1)}, u32[]{:S(2)}, u32[]{:S(2)}) async-start(bf16[4,68,1024]{2,1,0:T(8,128)(2,1)} %fusion.46), calls=%async_computation.5 | async-start | bytes 1179648 | tf_op jit(solution)/shard_map/all_to_all | solution.py:88
  186.3 141.6 %reduce-scatter.5.cloned.1.call-start = ((), (), s32[]{:S(2)}) async-start(), calls=%async_computation.16 | async-start | bytes 4718592 | tf_op jit(solution)/shard_map/reduce_scatter | solution.py:129
  221.8 5.7 %copy-start.4 = (bf16[4,68,1024]{2,1,0:T(8,128)(2,1)}, bf16[4,68,1024]{2,1,0:T(8,128)(2,1)S(1)}, u32[]{:S(2)}) copy-start(bf16[4,68,1024]{2,1,0:T(8,128)(2,1)S(1)} %all_to_all.41) | copy-start | bytes 1671172
  227.5 1.0 copy-start.7
  232.9 1.9 copy-start.1
  232.9 149.5 %reduce-scatter.7.cloned.1.call-start = ((), (), s32[]{:S(2)}) async-start(), calls=%async_computation.17 | async-start | bytes 4718592 | tf_op jit(solution)/shard_map/reduce_scatter | solution.py:132
  240.5 1.7 copy-start.2
  247.0 18.7 %all-to-all-start.3 = ((bf16[4,68,1024]{2,1,0:T(8,128)(2,1)}), bf16[4,68,1024]{2,1,0:T(8,128)(2,1)S(1)}, u32[]{:S(2)}, u32[]{:S(2)}) async-start(bf16[4,68,1024]{2,1,0:T(8,128)(2,1)} %fusion.49), calls=%async_computation.3 | async-start | bytes 1179648 | tf_op jit(solution)/shard_map/all_to_all | solution.py:67
  265.7 18.9 %all-to-all-start.7 = ((bf16[4,68,1024]{2,1,0:T(8,128)(2,1)}), bf16[4,68,1024]{2,1,0:T(8,128)(2,1)S(1)}, u32[]{:S(2)}, u32[]{:S(2)}) async-start(bf16[4,68,1024]{2,1,0:T(8,128)(2,1)} %fusion.40), calls=%async_computation.7 | async-start | bytes 1179648 | tf_op jit(solution)/shard_map/all_to_all | solution.py:88
Sparse Core Ops, SparseCore 0:
  9.9 39.2 all-gather.4
  51.1 36.5 all-gather.6
  89.6 36.5 all-gather.8
  128.0 36.5 all-gather.10
  167.8 51.1 reduce-scatter.10
  222.2 51.1 reduce-scatter.8
  276.7 51.1 reduce-scatter.4
  331.2 51.1 reduce-scatter.6
where the time goes:
time: 392 us; the launch traced here: 391 us
  waiting for transfers between devices  226 us (58%)
  matrix products  65.8 us (17%)
  blocking collectives  40 us (10%)
  starting transfers between devices  23.7 us (6%)
  between operations  14.5 us (4%)
  other arithmetic  12.4 us (3%)
  local copies, waits for them, and re-layouts  9.04 us (2%)
    reduce_scatter x1, waiting for transfers between devices, local(): lax.psum_scatter(down_grad_first.astype(jnp.bfloat16), 'dp', scatter_dime...  52.4 us
    reduce_scatter x1, waiting for transfers between devices, local(): lax.psum_scatter(up_grad_first.astype(jnp.bfloat16), 'dp', scatter_dimens...  37.3 us
    all_gather x2, waiting for transfers between devices, fetch_layer(): lax.all_gather(down_shard, 'dp', axis=1, tiled=True)  36.7 us
    all_to_all x2, waiting for transfers between devices, moe_backward(): lax.all_to_all(grad_slots, 'expert', split_axis=0, concat_axis=0, tiled=T...  30.5 us
    all_to_all x2, waiting for transfers between devices, moe_forward(): lax.all_to_all(partial_out, 'expert', split_axis=0, concat_axis=0, tiled=...  26.2 us
    all_to_all x1, blocking collectives, moe_forward(): lax.all_to_all(outgoing, 'expert', split_axis=0, concat_axis=0, tiled=True)  22 us
    all_to_all x1, blocking collectives, moe_backward(): lax.all_to_all(outgoing, 'expert', split_axis=0, concat_axis=0, tiled=True)  17.9 us
    all_to_all x1, waiting for transfers between devices, moe_forward(): lax.all_to_all(outgoing, 'expert', split_axis=0, concat_axis=0, tiled=True)  15.1 us
  transfers between devices with their start and end apart: 14, of which 11 were waited for; matrix products, arithmetic and copies ran while one was open for 20% of the time, Pallas kernels for 0%

commit v1 on v0

v1 whole, which is shorter than its diff:
```python
import functools

import jax
import jax.numpy as jnp
from jax import lax
from jax.experimental import pallas as pl
from jax.experimental.pallas import tpu as pltpu
from jax.sharding import PartitionSpec as P

epsilon = 1e-06


def rms_normal(widened):
    return widened * lax.rsqrt(jnp.mean(widened * widened, axis=-1, keepdims=True) + epsilon)


def gelu_slope(pre_gelu):
    _, pullback = jax.vjp(jax.nn.gelu, pre_gelu)
    return pullback(jnp.ones_like(pre_gelu))[0]


def slot_places(route_ids, experts, capacity):
    expert_ids = route_ids[:, 0]
    onehot = (expert_ids[:, None] == jnp.arange(experts, dtype=jnp.int32)[None, :]).astype(
        jnp.int32
    )
    earlier = jnp.cumsum(onehot, axis=0) - onehot
    return expert_ids * capacity + jnp.sum(earlier * onehot, axis=1)


def to_slots(token_rows, places, slot_count):
    onehot_table = (places[None, :] == jnp.arange(slot_count, dtype=jnp.int32)[:, None]).astype(
        token_rows.dtype
    )
    return jnp.dot(onehot_table, token_rows, preferred_element_type=jnp.float32).astype(
        token_rows.dtype
    )


def from_slots(returned, places, experts):
    group_size = returned.shape[0] // experts
    feature_count = returned.shape[2]
    summed = (
        returned.reshape(experts, group_size, returned.shape[1], feature_count)
        .astype(jnp.float32)
        .sum(axis=1)
    )
    summed = summed.reshape(-1, feature_count)
    onehot_table = (
        places[:, None] == jnp.arange(summed.shape[0], dtype=jnp.int32)[None, :]
    ).astype(jnp.float32)
    return jnp.dot(
        onehot_table, summed, precision=lax.Precision.HIGHEST, preferred_element_type=jnp.float32
    )


VMEM_LIMIT = 48 * 1024 * 1024


def comm_kernel(gather_rows, scatter_rows, exchange_slots, *refs):
    n_gather, n_scatter, n_exchange = len(gather_rows), len(scatter_rows), len(exchange_slots)
    refs = list(refs)

    def take(count):
        taken = refs[:count]
        del refs[:count]
        return taken

    shards, grads, outgoing = take(n_gather), take(n_scatter), take(n_exchange)
    fulls, sums, received = take(n_gather), take(n_scatter), take(n_exchange)
    scatter_scratch = [take(8) for _ in range(n_scatter)]
    send_sems, recv_sems, local_sems = take(3)
    used = [0, 0]

    dp = lax.axis_index("dp")
    z = lax.axis_index("expert")
    z_count = lax.axis_size("expert")
    core = lax.rem(dp, 2)
    x_bit = lax.rem(lax.div(dp, 2), 2)
    y_bit = lax.div(dp, 4)
    twin = dp + 1 - 2 * core
    x_side = dp + 2 - 4 * x_bit
    y_side = dp + 4 - 8 * y_bit
    diagonal = x_side + 4 - 8 * y_bit

    barrier = pltpu.get_barrier_semaphore()
    peers = 0
    if n_gather or n_scatter:
        for side in (twin, x_side, y_side):
            pl.semaphore_signal(
                barrier, inc=1, device_id=(side, z), device_id_type=pl.DeviceIdType.MESH
            )
            peers += 1
    if n_exchange:
        for step in range(1, z_count):
            pl.semaphore_signal(
                barrier,
                inc=1,
                device_id=(dp, lax.rem(z + step, z_count)),
                device_id_type=pl.DeviceIdType.MESH,
            )
            peers += 1
    pl.semaphore_wait(barrier, peers)

    def send(source, target, to_dp, to_z):
        index = used[0]
        used[0] += 1
        copy = pltpu.make_async_remote_copy(
            src_ref=source,
            dst_ref=target,
            send_sem=send_sems.at[index],
            recv_sem=recv_sems.at[index],
            device_id=(to_dp, to_z),
            device_id_type=pl.DeviceIdType.MESH,
        )
        copy.start()
        return copy

    def keep(source, target):
        index = used[1]
        used[1] += 1
        copy = pltpu.make_async_copy(source, target, local_sems.at[index])
        copy.start()
        return copy

    remote, local = [], []
    swaps = []
    for grad, rows, scratch in zip(grads, scatter_rows, scatter_scratch):
        from_twin = scratch[0]
        swap = []
        for slot, owner in enumerate((diagonal, x_side, y_side, dp)):
            theirs = owner + 1 - 2 * core
            part = grad.at[pl.ds(pl.multiple_of(theirs * rows, rows), rows), :]
            swap.append(send(part, from_twin.at[slot], twin, z))
        swaps.append(swap)

    for source, target, slots in zip(outgoing, received, exchange_slots):
        for step in range(1, z_count):
            to_z = lax.rem(z + step, z_count)
            slot = lax.div(to_z * slots, z_count)
            remote.append(send(source.at[slot], target.at[z], dp, to_z))
        local.append(keep(source.at[lax.div(z * slots, z_count)], target.at[z]))

    def rows_of(ref, owner, rows, start=0, count=None):
        offset = pl.multiple_of(owner * rows + start, rows if count is None else count)
        return ref.at[pl.ds(offset, rows if count is None else count), :]

    firsts = []
    for shard, full, rows in zip(shards, fulls, gather_rows):
        mine = rows_of(full, dp, rows)
        firsts.append((send(shard, mine, x_side, z), send(shard, mine, y_side, z)))
        remote.append(send(shard, mine, twin, z))
        local.append(keep(shard, mine))

    diagonals = []
    for full, rows, (along_x, along_y) in zip(fulls, gather_rows, firsts):
        half = rows // 2
        along_x.wait_recv()
        part = rows_of(full, x_side, rows, 0, half)
        lower = send(part, part, y_side, z)
        part = rows_of(full, x_side, rows)
        remote.append(send(part, part, twin, z))
        along_y.wait_recv()
        part = rows_of(full, y_side, rows, half, half)
        upper = send(part, part, x_side, z)
        part = rows_of(full, y_side, rows)
        remote.append(send(part, part, twin, z))
        along_x.wait_send()
        along_y.wait_send()
        diagonals.append((lower, upper))
    for full, rows, (lower, upper) in zip(fulls, gather_rows, diagonals):
        half = rows // 2
        lower.wait_recv()
        part = rows_of(full, diagonal, rows, 0, half)
        remote.append(send(part, part, twin, z))
        upper.wait_recv()
        part = rows_of(full, diagonal, rows, half, half)
        remote.append(send(part, part, twin, z))
        lower.wait_send()
        upper.wait_send()

    def wide(ref):
        return ref[...].astype(jnp.float32)

    halves = []
    for grad, rows, scratch, swap in zip(grads, scatter_rows, scatter_scratch, swaps):
        from_twin, to_diagonal, to_x, to_y, via_x, via_y, from_x, from_y = scratch
        half = rows // 2
        swap[0].wait_recv()
        to_diagonal[...] = (
            wide(rows_of(grad, diagonal, rows)) + wide(from_twin.at[0])
        ).astype(jnp.bfloat16)
        swap[1].wait_recv()
        to_x[...] = (wide(rows_of(grad, x_side, rows)) + wide(from_twin.at[1])).astype(
            jnp.bfloat16
        )
        low, high = pl.ds(0, half), pl.ds(half, half)
        relay_x = send(to_diagonal.at[low, :], via_x, x_side, z)
        relay_y = send(to_diagonal.at[high, :], via_y, y_side, z)
        swap[2].wait_recv()
        to_y[...] = (wide(rows_of(grad, y_side, rows)) + wide(from_twin.at[2])).astype(
            jnp.bfloat16
        )
        direct_x = send(to_x.at[low, :], from_x.at[low, :], x_side, z)
        direct_y = send(to_y.at[high, :], from_y.at[high, :], y_side, z)
        swap[3].wait_recv()
        halves.append((relay_x, relay_y, direct_x, direct_y))
    finals = []
    for rows, scratch, (relay_x, relay_y, direct_x, direct_y) in zip(
        scatter_rows, scatter_scratch, halves
    ):
        from_twin, to_diagonal, to_x, to_y, via_x, via_y, from_x, from_y = scratch
        half = rows // 2
        low, high = pl.ds(0, half), pl.ds(half, half)
        relay_y.wait_recv()
        to_x[high, :] = (wide(to_x.at[high, :]) + wide(via_y)).astype(jnp.bfloat16)
        relay_x.wait_recv()
        to_y[low, :] = (wide(to_y.at[low, :]) + wide(via_x)).astype(jnp.bfloat16)
        last_x = send(to_x.at[high, :], from_x.at[high, :], x_side, z)
        last_y = send(to_y.at[low, :], from_y.at[low, :], y_side, z)
        finals.append((last_x, last_y))
    for grad, total, rows, scratch, swap, pieces, last in zip(
        grads, sums, scatter_rows, scatter_scratch, swaps, halves, finals
    ):
        from_twin, to_diagonal, to_x, to_y, via_x, via_y, from_x, from_y = scratch
        for copy in pieces[2:] + last:
            copy.wait_recv()
        total[...] = (
            wide(rows_of(grad, dp, rows)) + wide(from_twin.at[3]) + wide(from_x) + wide(from_y)
        )
        for copy in tuple(swap) + pieces + last:
            copy.wait_send()
    for copy in remote:
        copy.wait()
    for copy in local:
        copy.wait()


def communicate(collective_id, gathers=(), scatters=(), exchanges=()):
    ways = lax.axis_size("dp")
    z_count = lax.axis_size("expert")
    if ways != 8:
        fulls = [lax.all_gather(shard, "dp", axis=0, tiled=True) for shard in gathers]
        sums = [
            lax.psum_scatter(grad, "dp", scatter_dimension=0, tiled=True).astype(jnp.float32)
            for grad in scatters
        ]
        received = [
            lax.all_to_all(
                jnp.repeat(slots, z_count // slots.shape[0], axis=0),
                "expert",
                split_axis=0,
                concat_axis=0,
                tiled=True,
            )
            for slots in exchanges
        ]
        return (*fulls, *sums, *received)
    outs, out_specs, scratch = [], [], []
    for shard in gathers:
        outs.append(jax.ShapeDtypeStruct((ways * shard.shape[0], shard.shape[1]), shard.dtype))
        out_specs.append(pl.BlockSpec(memory_space=pl.ANY))
    for grad in scatters:
        rows, columns = grad.shape[0] // ways, grad.shape[1]
        outs.append(jax.ShapeDtypeStruct((rows, columns), jnp.float32))
        out_specs.append(pl.BlockSpec(memory_space=pltpu.VMEM))
        scratch.append(pltpu.VMEM((4, rows, columns), grad.dtype))
        for height in (rows, rows, rows, rows // 2, rows // 2, rows, rows):
            scratch.append(pltpu.VMEM((height, columns), grad.dtype))
    for slots in exchanges:
        outs.append(jax.ShapeDtypeStruct((z_count, *slots.shape[1:]), slots.dtype))
        out_specs.append(pl.BlockSpec(memory_space=pl.ANY))
    copies = 9 * len(gathers) + 10 * len(scatters) + (z_count - 1) * len(exchanges)
    scratch += [
        pltpu.SemaphoreType.DMA((copies,)),
        pltpu.SemaphoreType.DMA((copies,)),
        pltpu.SemaphoreType.DMA((max(len(gathers) + len(exchanges), 1),)),
    ]
    inputs = (*gathers, *scatters, *exchanges)
    return pl.pallas_call(
        functools.partial(
            comm_kernel,
            tuple(shard.shape[0] for shard in gathers),
            tuple(grad.shape[0] // ways for grad in scatters),
            tuple(slots.shape[0] for slots in exchanges),
        ),
        out_shape=tuple(outs),
        in_specs=[pl.BlockSpec(memory_space=pltpu.VMEM)] * len(inputs),
        out_specs=tuple(out_specs),
        scratch_shapes=scratch,
        compiler_params=pltpu.CompilerParams(
            collective_id=collective_id, has_side_effects=True, vmem_limit_bytes=VMEM_LIMIT
        ),
        name="comm_%d" % collective_id,
    )(*inputs)


def slotted(token_rows, places, experts, capacity):
    return to_slots(token_rows, places, experts * capacity).reshape(experts, capacity, -1)


def project_up(received, up_full):
    pre_gelu = jnp.einsum("skd,dh->skh", received, up_full, preferred_element_type=jnp.float32)
    return pre_gelu, jax.nn.gelu(pre_gelu).astype(jnp.bfloat16)


def project_down(hidden, down_full):
    return jnp.einsum("skh,hd->skd", hidden, down_full, preferred_element_type=jnp.float32).astype(
        jnp.bfloat16
    )


def layer_gradients(arriving, received, pre_gelu, hidden, up_full, down_full):
    grad_hidden = jnp.einsum("skd,hd->skh", arriving, down_full, preferred_element_type=jnp.float32)
    grad_pre = (grad_hidden * gelu_slope(pre_gelu)).astype(jnp.bfloat16)
    grad_down = jnp.einsum("skh,skd->hd", hidden, arriving, preferred_element_type=jnp.float32)
    grad_up = jnp.einsum("skd,skh->dh", received, grad_pre, preferred_element_type=jnp.float32)
    grad_slots = jnp.einsum(
        "skh,dh->skd", grad_pre, up_full, preferred_element_type=jnp.float32
    ).astype(jnp.bfloat16)
    return grad_up.astype(jnp.bfloat16), grad_down.astype(jnp.bfloat16), grad_slots


def grad_through_norm(upstream, widened, grad_normed):
    _, pullback = jax.vjp(rms_normal, widened)
    return (upstream.astype(jnp.float32) + pullback(grad_normed)[0]).astype(jnp.bfloat16)


def capacity_for(token_count, experts):
    return min(token_count, (token_count * 17 + 16 * experts - 1) // (16 * experts))


def local(
    tokens, route_first, route_second, up_first, down_first, up_second, down_second, cotangent
):
    expert_devices = lax.axis_size("expert")
    token_count = tokens.shape[0]
    experts_first = max(expert_devices // 4, 2)
    experts_second = max(expert_devices // 2, 2)
    cap_first = capacity_for(token_count, experts_first)
    cap_second = capacity_for(token_count, experts_second)
    places_first = slot_places(route_first, experts_first, cap_first)
    places_second = slot_places(route_second, experts_second, cap_second)

    widened = tokens.astype(jnp.float32)
    normed_first = rms_normal(widened).astype(jnp.bfloat16)
    up_one, down_one, received_first, arriving_second = communicate(
        0,
        gathers=(up_first[0], down_first[0]),
        exchanges=(
            slotted(normed_first, places_first, experts_first, cap_first),
            slotted(cotangent, places_second, experts_second, cap_second),
        ),
    )
    pre_first, hidden_first = project_up(received_first, up_one)
    up_two, returned = communicate(
        1, gathers=(up_second[0],), exchanges=(project_down(hidden_first, down_one),)
    )
    middle = (widened + from_slots(returned, places_first, experts_first)).astype(jnp.bfloat16)
    middle_wide = middle.astype(jnp.float32)
    normed_second = rms_normal(middle_wide).astype(jnp.bfloat16)
    down_two, received_second = communicate(
        2,
        gathers=(down_second[0],),
        exchanges=(slotted(normed_second, places_second, experts_second, cap_second),),
    )
    pre_second, hidden_second = project_up(received_second, up_two)
    part_second = project_down(hidden_second, down_two)
    grad_up_two, grad_down_two, slot_grads = layer_gradients(
        arriving_second, received_second, pre_second, hidden_second, up_two, down_two
    )
    down_grad_second, coming_back = communicate(
        3, scatters=(grad_down_two,), exchanges=(slot_grads,)
    )
    grad_middle = grad_through_norm(
        cotangent, middle_wide, from_slots(coming_back, places_second, experts_second)
    )
    up_grad_second, arriving_first = communicate(
        4,
        scatters=(grad_up_two,),
        exchanges=(slotted(grad_middle, places_first, experts_first, cap_first),),
    )
    grad_up_one, grad_down_one, slot_grads = layer_gradients(
        arriving_first, received_first, pre_first, hidden_first, up_one, down_one
    )
    up_grad_first, down_grad_first, coming_back, returned = communicate(
        5, scatters=(grad_up_one, grad_down_one), exchanges=(slot_grads, part_second)
    )
    grad_tokens = grad_through_norm(
        grad_middle, widened, from_slots(coming_back, places_first, experts_first)
    )
    branch = from_slots(returned, places_second, experts_second)
    layer_out = (middle_wide + branch).astype(jnp.bfloat16)
    return (
        layer_out,
        grad_tokens,
        up_grad_first[None],
        down_grad_first[None],
        up_grad_second[None],
        down_grad_second[None],
    )


def solution(mesh):
    in_specs = (
        P(("dp", "expert"), None),
        P(("dp", "expert"), None),
        P(("dp", "expert"), None),
        P("expert", "dp", None),
        P("expert", "dp", None),
        P("expert", "dp", None),
        P("expert", "dp", None),
        P(("dp", "expert"), None),
    )
    out_specs = (
        P(("dp", "expert"), None),
        P(("dp", "expert"), None),
        P("expert", "dp", None),
        P("expert", "dp", None),
        P("expert", "dp", None),
        P("expert", "dp", None),
    )
    return jax.shard_map(local, mesh=mesh, in_specs=in_specs, out_specs=out_specs, check_vma=False)
```

time: 392 us -> 263 us (0.67)
  waiting for transfers between devices: 226 us -> 0 us
  Pallas kernels: 0 us -> 185 us
  blocking collectives: 40 us -> 0 us
  starting transfers between devices: 23.7 us -> 0 us
  matrix products: 65.8 us -> 48.3 us
  between operations: 14.5 us -> 1.06 us
  local copies, waits for them, and re-layouts: 9.04 us -> 14.7 us
    pallas_call x0 -> x6, Pallas kernels: none -> 185 us  [communicate(): pl.pallas_call(functools.partial(comm_kernel, tuple((shard.shape[0] for s...]
    reduce_scatter x4 -> x0, waiting for transfers between devices: 89.7 us -> none  [the longest x1 52.4 us: local(): lax.psum_scatter(down_grad_first.astype(jnp.bfloat16), 'dp', scatter_dime...]
    all_to_all x6 -> x0, waiting for transfers between devices: 82.1 us -> none  [the longest x2 30.5 us: moe_backward(): lax.all_to_all(grad_slots, 'expert', split_axis=0, concat_axis=0, tiled=T...]
    all_gather x4 -> x0, waiting for transfers between devices: 51.5 us -> none  [the longest x2 36.7 us: fetch_layer(): lax.all_gather(down_shard, 'dp', axis=1, tiled=True)]
    all_to_all x2 -> x0, blocking collectives: 40 us -> none  [the longest x1 22 us: moe_forward(): lax.all_to_all(outgoing, 'expert', split_axis=0, concat_axis=0, tiled=True)]
    all_to_all x6 -> x0, starting transfers between devices: 23.1 us -> none  [the longest x2 8.06 us: moe_backward(): lax.all_to_all(grad_slots, 'expert', split_axis=0, concat_axis=0, tiled=T...]
    dot_general x12, matrix products: 62 us -> 39.3 us  [the longest x2 9.23 us: layer_gradients(): jnp.einsum('skh,skd->hd', hidden, arriving, preferred_element_type=jnp.fl...]
    broadcast_in_dim x4 -> x0, other arithmetic: 8.57 us -> none  [the longest x2 4.32 us: local(): reduced_second = (reduced_all[2][None], reduced_all[3][None])]
  transfers between devices with their start and end apart: 14 -> 0, of which waited for: 11 -> 0; matrix products, arithmetic and copies ran while one was open for 20% -> 0% of each run, Pallas kernels for 0% -> 0%
where the time goes in v1:
time: 263 us; the launch traced here: 262 us
  Pallas kernels  185 us (70%)
  matrix products  48.3 us (18%)
  local copies, waits for them, and re-layouts  14.7 us (6%)
  other arithmetic  12.6 us (5%)
    pallas_call x6, Pallas kernels, communicate(): pl.pallas_call(functools.partial(comm_kernel, tuple((shard.shape[0] for s...  185 us
    dot_general x2, matrix products, layer_gradients(): jnp.einsum('skh,skd->hd', hidden, arriving, preferred_element_type=jnp.fl...  9.23 us
    unnamed x38, local copies, waits for them, and re-layouts  8.6 us
    dot_general x2, matrix products, layer_gradients(): jnp.einsum('skd,skh->dh', received, grad_pre, preferred_element_type=jnp....  7.97 us
    dot_general x2, matrix products, layer_gradients(): jnp.einsum('skd,hd->skh', arriving, down_full, preferred_element_type=jnp...  7.45 us
    dot_general x2, matrix products, project_up(): jnp.einsum('skd,dh->skh', received, up_full, preferred_element_type=jnp.f...  7.3 us
    dot_general x4, matrix products, from_slots(): jnp.dot(onehot_table, summed, precision=lax.Precision.HIGHEST, preferred_...  6.03 us
    reshape x4, local copies, waits for them, and re-layouts, from_slots(): summed = summed.reshape(-1, feature_count)  5.83 us

profile of v1, /device:TPU:0, one launch (start us, length us, event | category | flops | bytes accessed | tf_op | source)
XLA Modules:
  0.0 262.0 jit_solution(9367613625949754819)
XLA Ops:
  10.6 43.6 %comm_0.1 = (bf16[1024,2048]{1,0:T(8,128)(2,1)}, bf16[2048,1024]{1,0:T(8,128)(2,1)}, bf16[4,68,1024]{2,1,0:T(8,128)(2,1)S(1)}, bf16[4,68,1024]{2,1,0:T(8,128)(2,1)S(1)}) custom-call(bf16[128,2048]{1,0:T(8,128)(2,1)S(1)} %bitcast.102, bf16[256,1024]{1,0:T(8,128)(2,1)S(1)} %bitcast.103, bf16[2,68,1024]{2,1,0:T(8,128)(2,1)S(1)} %reshape.98.refs_2_, ...), custom_call_target="tpu_custom_call" | custom-call | tf_op jit(solution)/shard_map/comm_0/pallas_call | solution.py:280
  54.2 3.7 %fusion.14 = f32[4,68,2048]{2,1,0:T(8,128)S(1)} fusion(bf16[4,68,1024]{2,1,0:T(8,128)(2,1)S(1)} %get-tuple-element.22, bf16[1024,2048]{1,0:T(8,128)(2,1)} %get-tuple-element.23), kind=kOutput, calls=%fused_computation.18 | convolution fusion | flops 1140850688 | bytes 6979584 | tf_op jit(solution)/shard_map/skd,dh->skh/dot_general | solution.py:303
  58.0 1.8 fusion.43.refs_1_
  59.8 23.7 %comm_1.1 = (bf16[1024,2048]{1,0:T(8,128)(2,1)S(1)}, bf16[4,68,1024]{2,1,0:T(8,128)(2,1)S(1)}) custom-call(bf16[128,2048]{1,0:T(8,128)(2,1)S(1)} %bitcast.104, bf16[4,68,1024]{2,1,0:T(8,128)(2,1)S(1)} %fusion.43.refs_1_), custom_call_target="tpu_custom_call" | custom-call | tf_op jit(solution)/shard_map/comm_1/pallas_call | solution.py:280
  83.6 2.0 copy-done
  86.5 1.6 multiply_reduce_fusion.1
  88.5 24.5 %comm_2.1 = (bf16[2048,1024]{1,0:T(8,128)(2,1)S(1)}, bf16[4,68,1024]{2,1,0:T(8,128)(2,1)S(1)}) custom-call(bf16[256,1024]{1,0:T(8,128)(2,1)S(1)} %bitcast.105, bf16[2,68,1024]{2,1,0:T(8,128)(2,1)S(1)} %reshape.101.refs_1_), custom_call_target="tpu_custom_call" | custom-call | tf_op jit(solution)/shard_map/comm_2/pallas_call | solution.py:280
  113.0 3.6 %fusion.2 = f32[4,68,2048]{2,1,0:T(8,128)S(1)} fusion(bf16[4,68,1024]{2,1,0:T(8,128)(2,1)S(1)} %get-tuple-element.26, bf16[1024,2048]{1,0:T(8,128)(2,1)} %copy-done), kind=kOutput, calls=%fused_computation.6 | convolution fusion | flops 1140850688 | bytes 6979584 | tf_op jit(solution)/shard_map/skd,dh->skh/dot_general | solution.py:303
  116.6 2.7 %fusion.46.refs_3_ = bf16[4,68,1024]{2,1,0:T(8,128)(2,1)} fusion(bf16[2048,1024]{1,0:T(8,128)(2,1)S(1)} %get-tuple-element.28, f32[4,68,2048]{2,1,0:T(8,128)S(1)} %fusion.2), kind=kOutput, calls=%fused_computation.44 | convolution fusion | flops 1146142720 | bytes 6979584 | tf_op jit(solution)/shard_map/skh,hd->skd/dot_general | solution.py:308
  119.3 2.6 fusion.22
  123.4 4.6 %bitcast_convert_fusion.2.refs_0_ = bf16[2048,1024]{1,0:T(8,128)(2,1)} fusion(bf16[4,68,1024]{2,1,0:T(8,128)(2,1)S(1)} %get-tuple-element.27, f32[4,68,2048]{2,1,0:T(8,128)S(1)} %fusion.2), kind=kOutput, calls=%fused_computation.2 | convolution fusion | flops 1147961344 | bytes 6979584 | tf_op jit(solution)/shard_map/skh,skd->hd/dot_general | solution.py:316
  128.0 25.6 %comm_3.1 = (f32[256,1024]{1,0:T(8,128)S(1)}, bf16[4,68,1024]{2,1,0:T(8,128)(2,1)S(1)}) custom-call(bf16[2048,1024]{1,0:T(8,128)(2,1)} %bitcast_convert_fusion.2.refs_0_, bf16[4,68,1024]{2,1,0:T(8,128)(2,1)S(1)} %fusion.49.refs_1_), custom_call_target="tpu_custom_call" | custom-call | tf_op jit(solution)/shard_map/comm_3/pallas_call | solution.py:280
  158.0 3.7 %bitcast_convert_fusion.3.refs_0_ = bf16[1024,2048]{1,0:T(8,128)(2,1)S(1)} fusion(bf16[4,68,1024]{2,1,0:T(8,128)(2,1)S(1)} %get-tuple-element.26, bf16[4,68,2048]{2,1,0:T(8,128)(2,1)} %copy-done.16), kind=kOutput, calls=%fused_computation.3 | convolution fusion | flops 1142947840 | bytes 5865472 | tf_op jit(solution)/shard_map/skd,skh->dh/dot_general | solution.py:317
  161.7 24.1 %comm_4.1 = (f32[128,2048]{1,0:T(8,128)S(1)}, bf16[4,68,1024]{2,1,0:T(8,128)(2,1)S(1)}) custom-call(bf16[1024,2048]{1,0:T(8,128)(2,1)S(1)} %bitcast_convert_fusion.3.refs_0_, bf16[2,68,1024]{2,1,0:T(8,128)(2,1)S(1)} %reshape.103.refs_1_), custom_call_target="tpu_custom_call" | custom-call | tf_op jit(solution)/shard_map/comm_4/pallas_call | solution.py:280
  185.8 4.9 %fusion.25 = bf16[4,68,2048]{2,1,0:T(8,128)(2,1)S(1)} fusion(bf16[4,68,1024]{2,1,0:T(8,128)(2,1)S(1)} %get-tuple-element.31, bf16[2048,1024]{1,0:T(8,128)(2,1)} %get-tuple-element.24, f32[4,68,2048]{2,1,0:T(8,128)S(1)} %copy-done.13), kind=kOutput, calls=%fused_computation.27 | convolution fusion | flops 1151434752 | bytes 8093696 | tf_op jit(solution)/shard_map/skd,hd->skh/dot_general | solution.py:314
  192.1 4.6 %bitcast_convert_fusion.refs_1_ = bf16[2048,1024]{1,0:T(8,128)(2,1)} fusion(bf16[4,68,1024]{2,1,0:T(8,128)(2,1)S(1)} %get-tuple-element.31, f32[4,68,2048]{2,1,0:T(8,128)S(1)} %copy-done.13), kind=kOutput, calls=%fused_computation | convolution fusion | flops 1147961344 | bytes 6979584 | tf_op jit(solution)/shard_map/skh,skd->hd/dot_general | solution.py:316
  196.7 4.3 %bitcast_convert_fusion.1.refs_0_ = bf16[1024,2048]{1,0:T(8,128)(2,1)} fusion(bf16[4,68,1024]{2,1,0:T(8,128)(2,1)S(1)} %get-tuple-element.22, bf16[4,68,2048]{2,1,0:T(8,128)(2,1)S(1)} %fusion.25), kind=kOutput, calls=%fused_computation.1 | convolution fusion | flops 1142947840 | bytes 5865472 | tf_op jit(solution)/shard_map/skd,skh->dh/dot_general | solution.py:317
  201.0 43.9 %comm_5.1 = (f32[128,2048]{1,0:T(8,128)S(1)}, f32[256,1024]{1,0:T(8,128)S(1)}, bf16[4,68,1024]{2,1,0:T(8,128)(2,1)S(1)}, bf16[4,68,1024]{2,1,0:T(8,128)(2,1)S(1)}) custom-call(bf16[1024,2048]{1,0:T(8,128)(2,1)} %bitcast_convert_fusion.1.refs_0_, bf16[2048,1024]{1,0:T(8,128)(2,1)} %bitcast_convert_fusion.refs_1_, bf16[4,68,1024]{2,1,0:T(8,128)(2,1)S(1)} %fusion.40.refs_2_, ...), custom_call_target="tpu_custom_call" | custom-call | tf_op jit(solution)/shard_map/comm_5/pallas_call | solution.py:280
  247.2 1.9 reshape.105
  249.1 1.6 fusion.61
  250.7 1.9 fusion.58
  252.6 1.9 reshape.104
  254.5 2.3 fusion.54
  256.8 2.3 copy.18
  (68 shorter events, 23.6 us)
Async XLA Ops:
  0.6 9.9 %copy-start.5 = (bf16[1,256,1024]{2,1,0:T(8,128)(2,1)S(1)}, bf16[1,256,1024]{2,1,0:T(8,128)(2,1)}, u32[]{:S(2)}) copy-start(bf16[1,256,1024]{2,1,0:T(8,128)(2,1)} %param.12) | copy-start | bytes 1572868
  0.6 9.9 %copy-start.4 = (bf16[1,128,2048]{2,1,0:T(8,128)(2,1)S(1)}, bf16[1,128,2048]{2,1,0:T(8,128)(2,1)}, u32[]{:S(2)}) copy-start(bf16[1,128,2048]{2,1,0:T(8,128)(2,1)} %param.11) | copy-start | bytes 1572868
  54.2 3.7 %copy-start.15 = (bf16[2048,1024]{1,0:T(8,128)(2,1)S(1)}, bf16[2048,1024]{1,0:T(8,128)(2,1)}, u32[]{:S(2)}) copy-start(bf16[2048,1024]{1,0:T(8,128)(2,1)} %get-tuple-element.24) | copy-start | bytes 12582916
  58.0 1.9 copy-start.12
  58.0 1.9 copy-start.6
  59.8 26.7 %copy-start.9 = (bf16[128,1024]{1,0:T(8,128)(2,1)S(1)}, bf16[128,1024]{1,0:T(8,128)(2,1)}, u32[]{:S(2)}) copy-start(bf16[128,1024]{1,0:T(8,128)(2,1)} %param.8) | copy-start | bytes 786436
  83.6 2.0 copy-start
  85.5 3.0 %copy-start.7 = (bf16[1,256,1024]{2,1,0:T(8,128)(2,1)S(1)}, bf16[1,256,1024]{2,1,0:T(8,128)(2,1)}, u32[]{:S(2)}) copy-start(bf16[1,256,1024]{2,1,0:T(8,128)(2,1)} %param.14) | copy-start | bytes 1572868
  88.1 68.0 %copy-start.8 = (f32[128,1024]{1,0:T(8,128)}, f32[128,1024]{1,0:T(8,128)S(1)}, u32[]{:S(2)}) copy-start(f32[128,1024]{1,0:T(8,128)S(1)} %get-tuple-element.39) | copy-start | bytes 1572868
  119.3 2.6 copy-start.1
  121.9 1.5 copy-start.16
  157.3 0.7 copy-start.14
  161.6 24.1 %copy-start.13 = (f32[4,68,2048]{2,1,0:T(8,128)S(1)}, f32[4,68,2048]{2,1,0:T(8,128)}, u32[]{:S(2)}) copy-start(f32[4,68,2048]{2,1,0:T(8,128)} %copy-done.12) | copy-start | bytes 6684676
  185.8 4.9 %copy-start.11 = (bf16[1024,2048]{1,0:T(8,128)(2,1)S(1)}, bf16[1024,2048]{1,0:T(8,128)(2,1)}, u32[]{:S(2)}) copy-start(bf16[1024,2048]{1,0:T(8,128)(2,1)} %get-tuple-element.23) | copy-start | bytes 12582916
  196.7 4.3 %copy-start.3 = (bf16[4,68,1024]{2,1,0:T(8,128)(2,1)S(1)}, bf16[4,68,1024]{2,1,0:T(8,128)(2,1)}, u32[]{:S(2)}) copy-start(bf16[4,68,1024]{2,1,0:T(8,128)(2,1)} %fusion.46.refs_3_) | copy-start | bytes 1671172
  245.0 1.0 copy-start.2
  246.0 3.1 %copy-start.10 = (bf16[128,1024]{1,0:T(8,128)(2,1)S(1)}, bf16[128,1024]{1,0:T(8,128)(2,1)}, u32[]{:S(2)}) copy-start(bf16[128,1024]{1,0:T(8,128)(2,1)} %param.8) | copy-start | bytes 786436

commit v2 on v0

--- a/solution.py
+++ b/solution.py
@@ -1,6 +1,10 @@
+import functools
+
 import jax
 import jax.numpy as jnp
 from jax import lax
+from jax.experimental import pallas as pl
+from jax.experimental.pallas import tpu as pltpu
 from jax.sharding import PartitionSpec as P
 
 epsilon = 1e-06
@@ -104,7 +108,7 @@
     return min(token_count, (token_count * 17 + 16 * experts - 1) // (16 * experts))
 
 
-def local(
+def local_plain(
     tokens, route_first, route_second, up_first, down_first, up_second, down_second, cotangent
 ):
     expert_devices = lax.axis_size("expert")
@@ -151,6 +155,432 @@
     )
 
 
+VMEM_LIMIT = 56 * 1024 * 1024
+
+
+def block_tables(route, experts, capacity):
+    count = route.shape[0]
+    lanes = lax.broadcasted_iota(jnp.int32, (count, count), 1)
+    rows = lax.broadcasted_iota(jnp.int32, (count, count), 0)
+    onehot = jnp.where(lanes == route, 1.0, 0.0)
+    below = jnp.where(lanes < rows, 1.0, 0.0)
+    earlier = jnp.dot(
+        below.astype(jnp.bfloat16), onehot.astype(jnp.bfloat16), preferred_element_type=jnp.float32
+    )
+    place = jnp.sum(earlier * onehot, axis=1, keepdims=True).astype(jnp.int32)
+    slots = lax.broadcasted_iota(jnp.int32, (count, capacity), 1)
+    hit = jnp.where(slots == place, 1.0, 0.0)
+    return [
+        (hit * jnp.where(route == expert, 1.0, 0.0)).astype(jnp.bfloat16)
+        for expert in range(experts)
+    ]
+
+
+def fill_slots(target, tables, token_rows):
+    for expert, table in enumerate(tables):
+        target[expert] = lax.dot_general(
+            table, token_rows, (((0,), (0,)), ((), ())), preferred_element_type=jnp.float32
+        ).astype(target.dtype)
+
+
+def pick_up(parts, tables):
+    group_size = parts.shape[0] // len(tables)
+    total = None
+    for part in range(parts.shape[0]):
+        picked = jnp.dot(
+            tables[part // group_size], parts[part], preferred_element_type=jnp.float32
+        )
+        total = picked if total is None else total + picked
+    return total
+
+
+def add_norm_pullback(upstream, widened, grad_normed):
+    scale = lax.rsqrt(jnp.mean(widened * widened, axis=-1, keepdims=True) + epsilon)
+    along = jnp.mean(grad_normed * widened, axis=-1, keepdims=True)
+    pulled = scale * grad_normed - widened * (scale * scale * scale * along)
+    return (upstream.astype(jnp.float32) + pulled).astype(jnp.bfloat16)
+
+
+def stage_kernel(stage, experts_first, experts_second, capacities, *refs):
+    refs = list(refs)
+
+    def take(count):
+        taken = refs[:count]
+        del refs[:count]
+        return taken
+
+    cap_first, cap_second = capacities
+    gathering = stage < 2
+    shards, grads, fulls, sums, scatter_scratch = [], [], [], [], []
+    if gathering:
+        shards = take(2)
+    else:
+        grads = take(2)
+    if stage == 0:
+        route_first, route_second, tokens, cotangent = take(4)
+        *fulls, received, arriving, slots_one, slots_two = take(6)
+    elif stage == 1:
+        route_first, route_second, tokens, parts = take(4)
+        *fulls, received, middle, back, slots_one = take(6)
+    elif stage == 2:
+        route_first, route_second, cotangent, middle, parts = take(5)
+        *sums, arriving, grad_middle, back, slots_one = take(6)
+    else:
+        route_first, route_second, tokens, middle, grad_middle, parts, parts_second = take(7)
+        *sums, grad_tokens, layer_out, back, back_second = take(6)
+    if not gathering:
+        scatter_scratch = [take(8) for _ in grads]
+    gather_rows = [shard.shape[0] for shard in shards]
+    scatter_rows = [total.shape[0] for total in sums]
+    send_sems, recv_sems, local_sems = take(3)
+    used = [0, 0]
+
+    dp = lax.axis_index("dp")
+    z = lax.axis_index("expert")
+    z_count = lax.axis_size("expert")
+    core = lax.rem(dp, 2)
+    x_bit = lax.rem(lax.div(dp, 2), 2)
+    y_bit = lax.div(dp, 4)
+    twin = dp + 1 - 2 * core
+    x_side = dp + 2 - 4 * x_bit
+    y_side = dp + 4 - 8 * y_bit
+    diagonal = x_side + 4 - 8 * y_bit
+
+    barrier = pltpu.get_barrier_semaphore()
+    peers = 0
+    for side in (twin, x_side, y_side):
+        pl.semaphore_signal(
+            barrier, inc=1, device_id=(side, z), device_id_type=pl.DeviceIdType.MESH
+        )
+        peers += 1
+    for step in range(1, z_count):
+        pl.semaphore_signal(
+            barrier,
+            inc=1,
+            device_id=(dp, lax.rem(z + step, z_count)),
+            device_id_type=pl.DeviceIdType.MESH,
+        )
+        peers += 1
+    pl.semaphore_wait(barrier, peers)
+
+    def send(source, target, to_dp, to_z):
+        index = used[0]
+        used[0] += 1
+        copy = pltpu.make_async_remote_copy(
+            src_ref=source,
+            dst_ref=target,
+            send_sem=send_sems.at[index],
+            recv_sem=recv_sems.at[index],
+            device_id=(to_dp, to_z),
+            device_id_type=pl.DeviceIdType.MESH,
+        )
+        copy.start()
+        return copy
+
+    def keep(source, target):
+        index = used[1]
+        used[1] += 1
+        copy = pltpu.make_async_copy(source, target, local_sems.at[index])
+        copy.start()
+        return copy
+
+    remote, local = [], []
+    swaps = []
+    def rows_of(ref, owner, rows, start=0, count=None):
+        offset = pl.multiple_of(owner * rows + start, rows if count is None else count)
+        return ref.at[pl.ds(offset, rows if count is None else count), :]
+
+    def wide(ref):
+        return ref[...].astype(jnp.float32)
+
+    def exchange(source, target):
+        slots = source.shape[0]
+        copies = []
+        for step in range(1, z_count):
+            to_z = lax.rem(z + step, z_count)
+            slot = lax.div(to_z * slots, z_count)
+            copies.append(send(source.at[slot], target.at[z], dp, to_z))
+        copies.append(keep(source.at[lax.div(z * slots, z_count)], target.at[z]))
+        return copies
+
+    def finish(copies):
+        for copy in copies:
+            copy.wait()
+
+    for grad, rows, scratch in zip(grads, scatter_rows, scatter_scratch):
+        from_twin = scratch[0]
+        swap = []
+        for slot, owner in enumerate((diagonal, x_side, y_side, dp)):
+            theirs = owner + 1 - 2 * core
+            part = grad.at[pl.ds(pl.multiple_of(theirs * rows, rows), rows), :]
+            swap.append(send(part, from_twin.at[slot], twin, z))
+        swaps.append(swap)
+
+    if stage > 0:
+        returning = exchange(parts, back)
+    if stage == 3:
+        returning_second = exchange(parts_second, back_second)
+
+    firsts = []
+    for shard, full, rows in zip(shards, fulls, gather_rows):
+        mine = rows_of(full, dp, rows)
+        firsts.append((send(shard, mine, x_side, z), send(shard, mine, y_side, z)))
+        remote.append(send(shard, mine, twin, z))
+        local.append(keep(shard, mine))
+
+    halves = []
+    for grad, rows, scratch, swap in zip(grads, scatter_rows, scatter_scratch, swaps):
+        from_twin, to_diagonal, to_x, to_y, via_x, via_y, from_x, from_y = scratch
+        half = rows // 2
+        swap[0].wait_recv()
+        to_diagonal[...] = (
+            wide(rows_of(grad, diagonal, rows)) + wide(from_twin.at[0])
+        ).astype(jnp.bfloat16)
+        swap[1].wait_recv()
+        to_x[...] = (wide(rows_of(grad, x_side, rows)) + wide(from_twin.at[1])).astype(
+            jnp.bfloat16
+        )
+        low, high = pl.ds(0, half), pl.ds(half, half)
+        relay_x = send(to_diagonal.at[low, :], via_x, x_side, z)
+        relay_y = send(to_diagonal.at[high, :], via_y, y_side, z)
+        swap[2].wait_recv()
+        to_y[...] = (wide(rows_of(grad, y_side, rows)) + wide(from_twin.at[2])).astype(
+            jnp.bfloat16
+        )
+        direct_x = send(to_x.at[low, :], from_x.at[low, :], x_side, z)
+        direct_y = send(to_y.at[high, :], from_y.at[high, :], y_side, z)
+        swap[3].wait_recv()
+        halves.append((relay_x, relay_y, direct_x, direct_y))
+    first_tables = block_tables(route_first[...], experts_first, cap_first)
+    second_tables = block_tables(route_second[...], experts_second, cap_second)
+    if stage == 0:
+        normed = rms_normal(wide(tokens)).astype(jnp.bfloat16)
+        fill_slots(slots_one, first_tables, normed)
+        fill_slots(slots_two, second_tables, cotangent[...])
+        onward = exchange(slots_one, received) + exchange(slots_two, arriving)
+    elif stage == 1:
+        finish(returning)
+        middle_rows = (wide(tokens) + pick_up(back, first_tables)).astype(jnp.bfloat16)
+        normed = rms_normal(middle_rows.astype(jnp.float32)).astype(jnp.bfloat16)
+        fill_slots(slots_one, second_tables, normed)
+        middle[...] = middle_rows
+        onward = exchange(slots_one, received)
+    elif stage == 2:
+        finish(returning)
+        grad_rows = add_norm_pullback(
+            cotangent[...], wide(middle), pick_up(back, second_tables)
+        )
+        fill_slots(slots_one, first_tables, grad_rows)
+        grad_middle[...] = grad_rows
+        onward = exchange(slots_one, arriving)
+    else:
+        onward = []
+
+    diagonals = []
+    for full, rows, (along_x, along_y) in zip(fulls, gather_rows, firsts):
+        half = rows // 2
+        along_x.wait_recv()
+        part = rows_of(full, x_side, rows, 0, half)
+        lower = send(part, part, y_side, z)
+        part = rows_of(full, x_side, rows)
+        remote.append(send(part, part, twin, z))
+        along_y.wait_recv()
+        part = rows_of(full, y_side, rows, half, half)
+        upper = send(part, part, x_side, z)
+        part = rows_of(full, y_side, rows)
+        remote.append(send(part, part, twin, z))
+        along_x.wait_send()
+        along_y.wait_send()
+        diagonals.append((lower, upper))
+    for full, rows, (lower, upper) in zip(fulls, gather_rows, diagonals):
+        half = rows // 2
+        lower.wait_recv()
+        part = rows_of(full, diagonal, rows, 0, half)
+        remote.append(send(part, part, twin, z))
+        upper.wait_recv()
+        part = rows_of(full, diagonal, rows, half, half)
+        remote.append(send(part, part, twin, z))
+        lower.wait_send()
+        upper.wait_send()
+
+    finals = []
+    for rows, scratch, (relay_x, relay_y, direct_x, direct_y) in zip(
+        scatter_rows, scatter_scratch, halves
+    ):
+        from_twin, to_diagonal, to_x, to_y, via_x, via_y, from_x, from_y = scratch
+        half = rows // 2
+        low, high = pl.ds(0, half), pl.ds(half, half)
+        relay_y.wait_recv()
+        to_x[high, :] = (wide(to_x.at[high, :]) + wide(via_y)).astype(jnp.bfloat16)
+        relay_x.wait_recv()
+        to_y[low, :] = (wide(to_y.at[low, :]) + wide(via_x)).astype(jnp.bfloat16)
+        last_x = send(to_x.at[high, :], from_x.at[high, :], x_side, z)
+        last_y = send(to_y.at[low, :], from_y.at[low, :], y_side, z)
+        finals.append((last_x, last_y))
+    if stage == 3:
+        finish(returning)
+        grad_tokens[...] = add_norm_pullback(
+            grad_middle[...], wide(tokens), pick_up(back, first_tables)
+        )
+        finish(returning_second)
+        layer_out[...] = (wide(middle) + pick_up(back_second, second_tables)).astype(jnp.bfloat16)
+    for grad, total, rows, scratch, swap, pieces, last in zip(
+        grads, sums, scatter_rows, scatter_scratch, swaps, halves, finals
+    ):
+        from_twin, to_diagonal, to_x, to_y, via_x, via_y, from_x, from_y = scratch
+        for copy in pieces[2:] + last:
+            copy.wait_recv()
+        total[...] = (
+            wide(rows_of(grad, dp, rows)) + wide(from_twin.at[3]) + wide(from_x) + wide(from_y)
+        )
+        for copy in tuple(swap) + pieces + last:
+            copy.wait_send()
+    finish(onward)
+    finish(remote)
+    finish(local)
+
+
+def run_stage(stage, experts_first, experts_second, capacities, matrices, others, outs, slotted):
+    ways = lax.axis_size("dp")
+    z_count = lax.axis_size("expert")
+    shapes, out_specs = [], []
+    scratch = [pltpu.VMEM(shape, jnp.bfloat16) for shape in slotted]
+    for matrix in matrices:
+        if stage < 2:
+            shapes.append(
+                jax.ShapeDtypeStruct((ways * matrix.shape[0], matrix.shape[1]), matrix.dtype)
+            )
+            out_specs.append(pl.BlockSpec(memory_space=pl.ANY))
+        else:
+            rows, columns = matrix.shape[0] // ways, matrix.shape[1]
+            shapes.append(jax.ShapeDtypeStruct((rows, columns), jnp.float32))
+            out_specs.append(pl.BlockSpec(memory_space=pltpu.VMEM))
+            scratch.append(pltpu.VMEM((4, rows, columns), matrix.dtype))
+            for height in (rows, rows, rows, rows // 2, rows // 2, rows, rows):
+                scratch.append(pltpu.VMEM((height, columns), matrix.dtype))
+    for shape, in_vmem in outs:
+        shapes.append(jax.ShapeDtypeStruct(shape, jnp.bfloat16))
+        out_specs.append(pl.BlockSpec(memory_space=pltpu.VMEM if in_vmem else pl.ANY))
+    copies = 10 * len(matrices) + 2 * (z_count - 1)
+    scratch += [
+        pltpu.SemaphoreType.DMA((copies,)),
+        pltpu.SemaphoreType.DMA((copies,)),
+        pltpu.SemaphoreType.DMA((len(matrices) + 2,)),
+    ]
+    inputs = (*matrices, *others)
+    return pl.pallas_call(
+        functools.partial(stage_kernel, stage, experts_first, experts_second, capacities),
+        out_shape=tuple(shapes),
+        in_specs=[pl.BlockSpec(memory_space=pltpu.VMEM)] * len(inputs),
+        out_specs=tuple(out_specs),
+        scratch_shapes=scratch,
+        compiler_params=pltpu.CompilerParams(
+            collective_id=stage, has_side_effects=True, vmem_limit_bytes=VMEM_LIMIT
+        ),
+        name="stage_%d" % stage,
+    )(*inputs)
+
+
+def project_up(received, up_full):
+    pre_gelu = jnp.einsum("skd,dh->skh", received, up_full, preferred_element_type=jnp.float32)
+    return pre_gelu, jax.nn.gelu(pre_gelu).astype(jnp.bfloat16)
+
+
+def project_down(hidden, down_full):
+    return jnp.einsum("skh,hd->skd", hidden, down_full, preferred_element_type=jnp.float32).astype(
+        jnp.bfloat16
+    )
+
+
+def layer_gradients(arriving, received, pre_gelu, hidden, up_full, down_full):
+    grad_hidden = jnp.einsum("skd,hd->skh", arriving, down_full, preferred_element_type=jnp.float32)
+    grad_pre = (grad_hidden * gelu_slope(pre_gelu)).astype(jnp.bfloat16)
+    grad_down = jnp.einsum("skh,skd->hd", hidden, arriving, preferred_element_type=jnp.float32)
+    grad_up = jnp.einsum("skd,skh->dh", received, grad_pre, preferred_element_type=jnp.float32)
+    grad_slots = jnp.einsum(
+        "skh,dh->skd", grad_pre, up_full, preferred_element_type=jnp.float32
+    ).astype(jnp.bfloat16)
+    return grad_up.astype(jnp.bfloat16), grad_down.astype(jnp.bfloat16), grad_slots
+
+
+def local(
+    tokens, route_first, route_second, up_first, down_first, up_second, down_second, cotangent
+):
+    arguments = (
+        tokens,
+        route_first,
+        route_second,
+        up_first,
+        down_first,
+        up_second,
+        down_second,
+        cotangent,
+    )
+    z_count = lax.axis_size("expert")
+    if lax.axis_size("dp") != 8:
+        return local_plain(*arguments)
+    rows, width = tokens.shape
+    experts_first = max(z_count // 4, 2)
+    experts_second = max(z_count // 2, 2)
+    cap_first = -(-capacity_for(rows, experts_first) // 8) * 8
+    cap_second = -(-capacity_for(rows, experts_second) // 8) * 8
+    sizes = (experts_first, experts_second, (cap_first, cap_second))
+    outgoing_first = (experts_first, cap_first, width)
+    outgoing_second = (experts_second, cap_second, width)
+    incoming_first = (z_count, cap_first, width)
+    incoming_second = (z_count, cap_second, width)
+
+    up_one, down_one, received_first, arriving_second = run_stage(
+        0,
+        *sizes,
+        (up_first[0], down_first[0]),
+        (route_first, route_second, tokens, cotangent),
+        ((incoming_first, False), (incoming_second, False)),
+        (outgoing_first, outgoing_second),
+    )
+    pre_first, hidden_first = project_up(received_first, up_one)
+    up_two, down_two, received_second, middle = run_stage(
+        1,
+        *sizes,
+        (up_second[0], down_second[0]),
+        (route_first, route_second, tokens, project_down(hidden_first, down_one)),
+        ((incoming_second, False), (tokens.shape, True)),
+        (incoming_first, outgoing_second),
+    )
+    pre_second, hidden_second = project_up(received_second, up_two)
+    part_second = project_down(hidden_second, down_two)
+    grad_up_two, grad_down_two, slot_grads = layer_gradients(
+        arriving_second, received_second, pre_second, hidden_second, up_two, down_two
+    )
+    up_grad_second, down_grad_second, arriving_first, grad_middle = run_stage(
+        2,
+        *sizes,
+        (grad_up_two, grad_down_two),
+        (route_first, route_second, cotangent, middle, slot_grads),
+        ((incoming_first, False), (tokens.shape, True)),
+        (incoming_second, outgoing_first),
+    )
+    grad_up_one, grad_down_one, slot_grads = layer_gradients(
+        arriving_first, received_first, pre_first, hidden_first, up_one, down_one
+    )
+    up_grad_first, down_grad_first, grad_tokens, layer_out = run_stage(
+        3,
+        *sizes,
+        (grad_up_one, grad_down_one),
+        (route_first, route_second, tokens, middle, grad_middle, slot_grads, part_second),
+        ((tokens.shape, True), (tokens.shape, True)),
+        (incoming_first, incoming_second),
+    )
+    return (
+        layer_out,
+        grad_tokens,
+        up_grad_first[None],
+        down_grad_first[None],
+        up_grad_second[None],
+        down_grad_second[None],
+    )
+
+
 def solution(mesh):
     in_specs = (
         P(("dp", "expert"), None),

time: 392 us -> 233 us (0.59)
  waiting for transfers between devices: 226 us -> 0 us
  Pallas kernels: 0 us -> 179 us
  blocking collectives: 40 us -> 0 us
  matrix products: 65.8 us -> 42 us
  starting transfers between devices: 23.7 us -> 0 us
  between operations: 14.5 us -> 0.78 us
  other arithmetic: 12.4 us -> 0 us
    pallas_call x0 -> x4, Pallas kernels: none -> 179 us  [run_stage(): pl.pallas_call(functools.partial(stage_kernel, stage, experts_first, expe...]
    reduce_scatter x4 -> x0, waiting for transfers between devices: 89.7 us -> none  [the longest x1 52.4 us: local(): lax.psum_scatter(down_grad_first.astype(jnp.bfloat16), 'dp', scatter_dime...]
    all_to_all x6 -> x0, waiting for transfers between devices: 82.1 us -> none  [the longest x2 30.5 us: moe_backward(): lax.all_to_all(grad_slots, 'expert', split_axis=0, concat_axis=0, tiled=T...]
    all_gather x4 -> x0, waiting for transfers between devices: 51.5 us -> none  [the longest x2 36.7 us: fetch_layer(): lax.all_gather(down_shard, 'dp', axis=1, tiled=True)]
    all_to_all x2 -> x0, blocking collectives: 40 us -> none  [the longest x1 22 us: moe_forward(): lax.all_to_all(outgoing, 'expert', split_axis=0, concat_axis=0, tiled=True)]
    dot_general x20 -> x12, matrix products: 65.8 us -> 42 us  [the longest x2 9.17 us: layer_gradients(): jnp.einsum('skh,skd->hd', hidden, arriving, preferred_element_type=jnp.fl...]
    all_to_all x6 -> x0, starting transfers between devices: 23.1 us -> none  [the longest x2 8.06 us: moe_backward(): lax.all_to_all(grad_slots, 'expert', split_axis=0, concat_axis=0, tiled=T...]
    broadcast_in_dim x4 -> x0, other arithmetic: 8.57 us -> none  [the longest x2 4.32 us: local(): reduced_second = (reduced_all[2][None], reduced_all[3][None])]
  transfers between devices with their start and end apart: 14 -> 0, of which waited for: 11 -> 0; matrix products, arithmetic and copies ran while one was open for 20% -> 0% of each run, Pallas kernels for 0% -> 0%
where the time goes in v2:
time: 233 us
  Pallas kernels  179 us (77%)
  matrix products  42 us (18%)
  local copies, waits for them, and re-layouts  11.5 us (5%)
    pallas_call x4, Pallas kernels, run_stage(): pl.pallas_call(functools.partial(stage_kernel, stage, experts_first, expe...  179 us
    unnamed x30, local copies, waits for them, and re-layouts  11.5 us
    dot_general x2, matrix products, layer_gradients(): jnp.einsum('skh,skd->hd', hidden, arriving, preferred_element_type=jnp.fl...  9.17 us
    dot_general x2, matrix products, layer_gradients(): jnp.einsum('skd,skh->dh', received, grad_pre, preferred_element_type=jnp....  8.74 us
    dot_general x2, matrix products, project_up(): jnp.einsum('skd,dh->skh', received, up_full, preferred_element_type=jnp.f...  7.81 us
    dot_general x2, matrix products, layer_gradients(): jnp.einsum('skd,hd->skh', arriving, down_full, preferred_element_type=jnp...  6.37 us
    dot_general x2, matrix products, project_down(): jnp.einsum('skh,hd->skd', hidden, down_full, preferred_element_type=jnp.f...  5.4 us

profile of v2, /device:TPU:0, one launch (start us, length us, event | category | flops | bytes accessed | tf_op | source)
XLA Modules:
  0.0 233.0 jit_solution(4639214606919193913)
XLA Ops:
  0.6 1.4 copy.14.refs_2_
  2.0 1.4 copy.15.refs_3_
  3.4 44.6 %stage_0.1 = (bf16[1024,2048]{1,0:T(8,128)(2,1)}, bf16[2048,1024]{1,0:T(8,128)(2,1)}, bf16[4,72,1024]{2,1,0:T(8,128)(2,1)}, bf16[4,72,1024]{2,1,0:T(8,128)(2,1)}) custom-call(bf16[128,2048]{1,0:T(8,128)(2,1)} %bitcast.68, bf16[256,1024]{1,0:T(8,128)(2,1)} %bitcast.69, s32[128,1]{1,0:T(8,128)} %copy.14.refs_2_, s32[128,1]{1,0:T(8,128)} %copy.15.refs_3_, ...), custom_call_target="tpu_custom_call" | custom-call | tf_op jit(solution)/shard_map/stage_0/pallas_call | solution.py:471
  48.0 3.9 %fusion.14 = f32[4,72,2048]{2,1,0:T(8,128)S(1)} fusion(bf16[4,72,1024]{2,1,0:T(8,128)(2,1)} %get-tuple-element.22, bf16[1024,2048]{1,0:T(8,128)(2,1)} %get-tuple-element.23), kind=kOutput, calls=%fused_computation.18 | convolution fusion | flops 1207959552 | bytes 7143424 | tf_op jit(solution)/shard_map/skd,dh->skh/dot_general | solution.py:485
  51.9 2.7 %fusion.43.refs_5_ = bf16[4,72,1024]{2,1,0:T(8,128)(2,1)} fusion(bf16[2048,1024]{1,0:T(8,128)(2,1)S(1)} %copy-done.7, f32[4,72,2048]{2,1,0:T(8,128)S(1)} %fusion.14), kind=kOutput, calls=%fused_computation.43 | convolution fusion | flops 1213562880 | bytes 7143424 | tf_op jit(solution)/shard_map/skh,hd->skd/dot_general | solution.py:490
  54.6 41.6 %stage_1.1 = (bf16[1024,2048]{1,0:T(8,128)(2,1)}, bf16[2048,1024]{1,0:T(8,128)(2,1)}, bf16[4,72,1024]{2,1,0:T(8,128)(2,1)}, bf16[128,1024]{1,0:T(8,128)(2,1)}) custom-call(bf16[128,2048]{1,0:T(8,128)(2,1)} %bitcast.70, bf16[256,1024]{1,0:T(8,128)(2,1)} %bitcast.71, s32[128,1]{1,0:T(8,128)} %copy.14.refs_2_, s32[128,1]{1,0:T(8,128)} %copy.15.refs_3_, ...), custom_call_target="tpu_custom_call" | custom-call | tf_op jit(solution)/shard_map/stage_1/pallas_call | solution.py:471
  96.2 3.9 %fusion.2 = f32[4,72,2048]{2,1,0:T(8,128)S(1)} fusion(bf16[4,72,1024]{2,1,0:T(8,128)(2,1)} %get-tuple-element.25, bf16[1024,2048]{1,0:T(8,128)(2,1)} %get-tuple-element.28), kind=kOutput, calls=%fused_computation.6 | convolution fusion | flops 1207959552 | bytes 7143424 | tf_op jit(solution)/shard_map/skd,dh->skh/dot_general | solution.py:485
  100.1 2.7 %fusion.46.refs_8_ = bf16[4,72,1024]{2,1,0:T(8,128)(2,1)} fusion(bf16[2048,1024]{1,0:T(8,128)(2,1)S(1)} %copy-done.8, f32[4,72,2048]{2,1,0:T(8,128)S(1)} %fusion.2), kind=kOutput, calls=%fused_computation.44 | convolution fusion | flops 1213562880 | bytes 7143424 | tf_op jit(solution)/shard_map/skh,hd->skd/dot_general | solution.py:490
  102.8 2.6 %fusion.22 = bf16[4,72,2048]{2,1,0:T(8,128)(2,1)S(1)} fusion(bf16[4,72,1024]{2,1,0:T(8,128)(2,1)S(1)} %copy-done.9, bf16[2048,1024]{1,0:T(8,128)(2,1)S(1)} %copy-done.8, f32[4,72,2048]{2,1,0:T(8,128)S(1)} %fusion.2), kind=kOutput, calls=%fused_computation.26 | convolution fusion | flops 1219166208 | bytes 8323072 | tf_op jit(solution)/shard_map/skd,hd->skh/dot_general | solution.py:496
  105.5 2.3 fusion.49.refs_6_
  107.7 4.6 %bitcast_convert_fusion.2.refs_1_ = bf16[2048,1024]{1,0:T(8,128)(2,1)} fusion(bf16[4,72,1024]{2,1,0:T(8,128)(2,1)S(1)} %copy-done.9, f32[4,72,2048]{2,1,0:T(8,128)S(1)} %fusion.2), kind=kOutput, calls=%fused_computation.2 | convolution fusion | flops 1215365120 | bytes 7143424 | tf_op jit(solution)/shard_map/skh,skd->hd/dot_general | solution.py:498
  112.3 4.4 %bitcast_convert_fusion.3.refs_0_ = bf16[1024,2048]{1,0:T(8,128)(2,1)} fusion(bf16[4,72,1024]{2,1,0:T(8,128)(2,1)S(1)} %copy-done.6, bf16[4,72,2048]{2,1,0:T(8,128)(2,1)S(1)} %fusion.22), kind=kOutput, calls=%fused_computation.3 | convolution fusion | flops 1210056704 | bytes 5963776 | tf_op jit(solution)/shard_map/skd,skh->dh/dot_general | solution.py:499
  116.7 47.0 %stage_2.1 = (f32[128,2048]{1,0:T(8,128)}, f32[256,1024]{1,0:T(8,128)}, bf16[4,72,1024]{2,1,0:T(8,128)(2,1)}, bf16[128,1024]{1,0:T(8,128)(2,1)}) custom-call(bf16[1024,2048]{1,0:T(8,128)(2,1)} %bitcast_convert_fusion.3.refs_0_, bf16[2048,1024]{1,0:T(8,128)(2,1)} %bitcast_convert_fusion.2.refs_1_, s32[128,1]{1,0:T(8,128)} %copy.14.refs_2_, ...), custom_call_target="tpu_custom_call" | custom-call | tf_op jit(solution)/shard_map/stage_2/pallas_call | solution.py:471
  163.7 3.8 %fusion.25 = bf16[4,72,2048]{2,1,0:T(8,128)(2,1)S(1)} fusion(bf16[4,72,1024]{2,1,0:T(8,128)(2,1)} %get-tuple-element.30, bf16[2048,1024]{1,0:T(8,128)(2,1)S(1)} %copy-done.7, f32[4,72,2048]{2,1,0:T(8,128)S(1)} %fusion.14), kind=kOutput, calls=%fused_computation.27 | convolution fusion | flops 1219166208 | bytes 8323072 | tf_op jit(solution)/shard_map/skd,hd->skh/dot_general | solution.py:496
  167.5 2.3 fusion.40.refs_7_
  169.8 4.6 %bitcast_convert_fusion.refs_1_ = bf16[2048,1024]{1,0:T(8,128)(2,1)} fusion(bf16[4,72,1024]{2,1,0:T(8,128)(2,1)S(1)} %copy-done.10, f32[4,72,2048]{2,1,0:T(8,128)S(1)} %fusion.14), kind=kOutput, calls=%fused_computation | convolution fusion | flops 1215365120 | bytes 7143424 | tf_op jit(solution)/shard_map/skh,skd->hd/dot_general | solution.py:498
  174.4 4.4 %bitcast_convert_fusion.1.refs_0_ = bf16[1024,2048]{1,0:T(8,128)(2,1)} fusion(bf16[4,72,1024]{2,1,0:T(8,128)(2,1)S(1)} %copy-done.5, bf16[4,72,2048]{2,1,0:T(8,128)(2,1)S(1)} %fusion.25), kind=kOutput, calls=%fused_computation.1 | convolution fusion | flops 1210056704 | bytes 5963776 | tf_op jit(solution)/shard_map/skd,skh->dh/dot_general | solution.py:499
  178.8 45.5 %stage_3.1 = (f32[128,2048]{1,0:T(8,128)}, f32[256,1024]{1,0:T(8,128)}, bf16[128,1024]{1,0:T(8,128)(2,1)}, bf16[128,1024]{1,0:T(8,128)(2,1)}) custom-call(bf16[1024,2048]{1,0:T(8,128)(2,1)} %bitcast_convert_fusion.1.refs_0_, bf16[2048,1024]{1,0:T(8,128)(2,1)} %bitcast_convert_fusion.refs_1_, s32[128,1]{1,0:T(8,128)} %copy.14.refs_2_, ...), custom_call_target="tpu_custom_call" | custom-call | tf_op jit(solution)/shard_map/stage_3/pallas_call | solution.py:471
  224.3 1.8 copy.28
  226.0 1.8 copy.29
  227.8 2.3 copy.30
  230.1 1.0 copy.31
  231.1 1.0 copy.32
  232.0 1.0 copy.33
  (22 shorter events, 0.0 us)
Async XLA Ops:
  48.0 3.9 %copy-start.7 = (bf16[2048,1024]{1,0:T(8,128)(2,1)S(1)}, bf16[2048,1024]{1,0:T(8,128)(2,1)}, u32[]{:S(2)}) copy-start(bf16[2048,1024]{1,0:T(8,128)(2,1)} %get-tuple-element.24) | copy-start | bytes 12582916
  96.2 3.9 %copy-start.8 = (bf16[2048,1024]{1,0:T(8,128)(2,1)S(1)}, bf16[2048,1024]{1,0:T(8,128)(2,1)}, u32[]{:S(2)}) copy-start(bf16[2048,1024]{1,0:T(8,128)(2,1)} %get-tuple-element.27) | copy-start | bytes 12582916
  100.1 2.7 %copy-start.9 = (bf16[4,72,1024]{2,1,0:T(8,128)(2,1)S(1)}, bf16[4,72,1024]{2,1,0:T(8,128)(2,1)}, u32[]{:S(2)}) copy-start(bf16[4,72,1024]{2,1,0:T(8,128)(2,1)} %get-tuple-element.26) | copy-start | bytes 1769476
  102.8 2.6 %copy-start.1 = (bf16[1024,2048]{1,0:T(8,128)(2,1)S(1)}, bf16[1024,2048]{1,0:T(8,128)(2,1)}, u32[]{:S(2)}) copy-start(bf16[1024,2048]{1,0:T(8,128)(2,1)} %get-tuple-element.28) | copy-start | bytes 12582916
  107.7 4.6 %copy-start.6 = (bf16[4,72,1024]{2,1,0:T(8,128)(2,1)S(1)}, bf16[4,72,1024]{2,1,0:T(8,128)(2,1)}, u32[]{:S(2)}) copy-start(bf16[4,72,1024]{2,1,0:T(8,128)(2,1)} %get-tuple-element.25) | copy-start | bytes 1769476
  163.7 3.8 %copy-start = (bf16[1024,2048]{1,0:T(8,128)(2,1)S(1)}, bf16[1024,2048]{1,0:T(8,128)(2,1)}, u32[]{:S(2)}) copy-start(bf16[1024,2048]{1,0:T(8,128)(2,1)} %get-tuple-element.23) | copy-start | bytes 12582916
  167.5 2.3 copy-start.10
  169.8 4.6 %copy-start.5 = (bf16[4,72,1024]{2,1,0:T(8,128)(2,1)S(1)}, bf16[4,72,1024]{2,1,0:T(8,128)(2,1)}, u32[]{:S(2)}) copy-start(bf16[4,72,1024]{2,1,0:T(8,128)(2,1)} %get-tuple-element.22) | copy-start | bytes 1769476
  224.3 5.8 %copy-start.4 = (f32[256,1024]{1,0:T(8,128)S(1)}, f32[256,1024]{1,0:T(8,128)}, u32[]{:S(2)}) copy-start(f32[256,1024]{1,0:T(8,128)} %get-tuple-element.35) | copy-start | bytes 3145732
  226.0 5.0 %copy-start.3 = (f32[128,2048]{1,0:T(8,128)S(1)}, f32[128,2048]{1,0:T(8,128)}, u32[]{:S(2)}) copy-start(f32[128,2048]{1,0:T(8,128)} %get-tuple-element.36) | copy-start | bytes 3145732
  230.1 1.9 copy-start.2
